TPU v7x, 32 devices: a whole 2x2x4 slice. The times are simulated.
32 devices in a mesh: dom: 16 (over z, y, x), mem: 2 (over core).
Axes of the slice: x: 2, y: 2, z: 4, core: 2. Of those that a mesh axis runs over, the one named last changes fastest.
Arguments:
- node_latents: bfloat16 [4, 2048, 512], P('mem', 'dom'), may hold values from -6 to 6
- edge_latents: bfloat16 [4, 8192, 512], P('mem', 'dom'), may hold values from -6 to 6
- edge_senders: int32 [8192], P('dom'), may hold values from 0 to 191, as said below
- edge_receivers: int32 [8192], P('dom'), may hold values from 0 to 127
- edge_counts: int32 [16], P('dom'), may hold values from 64 to 512, as said below
- halo_send: int32 [512], P('dom'), may hold values from 0 to 127
- long_send: int32 [16, 16, 2], replicated, may hold values from 0 to 3
- edge_first: bfloat16 [2, 1536, 512], P(None, None, 'mem'), may hold values from -0.15625 to 0.15625
- edge_second: bfloat16 [2, 512, 512], P(None, None, 'mem'), may hold values from -0.25 to 0.25
- node_first: bfloat16 [2, 1024, 512], P(None, None, 'mem'), may hold values from -0.1875 to 0.1875
- node_second: bfloat16 [2, 512, 512], P(None, None, 'mem'), may hold values from -0.25 to 0.25
- edge_gain: float32 [2, 512], replicated, may hold values from 0.5 to 1.5
- edge_shift: float32 [2, 512], replicated, may hold values from -3 to 3
- node_gain: float32 [2, 512], replicated, may hold values from 0.5 to 1.5
- node_shift: float32 [2, 512], replicated, may hold values from -3 to 3
Outputs:
- node_out: bfloat16 [4, 2048, 512], P('mem', 'dom')
- edge_out: bfloat16 [4, 8192, 512], P('mem', 'dom')
Inputs may be any that keep to these rules, and one draw needn't show every extreme that they name: `edge_senders`: rows below 128 are the partition's own nodes, the next 32 its neighbours' sent nodes, the rest the coarse slots of all partitions. `edge_counts`: live slots come first in each partition; some partition has exactly 512 live slots.
All inputs are finite; a program needn't handle non-finite values.
Results may differ from a plain program's by a relative error of at most 0.0075.
Values may be sent and summed in bfloat16 or wider, within the bound.
A program may use at most 128 MiB of HBM per device.

v0:
```python
import functools

import jax
import jax.numpy as jnp
from jax import lax
from jax.experimental import pallas as pl
from jax.experimental.pallas import tpu as pltpu
from jax.sharding import PartitionSpec as P

F32, BF16 = jnp.float32, jnp.bfloat16
LANES = 128
CHUNK = 256


def round_up(value, step):
    return (value + step - 1) // step * step


def dot(a, b):
    return jnp.dot(a, b, preferred_element_type=F32)


def silu(x):
    half = 0.5 * x
    return (half + half * jnp.tanh(half)).astype(BF16)


def norm(x, gain, shift):
    average = jnp.mean(x, -1, keepdims=True)
    centred = x - average
    variance = jnp.mean(centred * centred, -1, keepdims=True)
    return centred * lax.rsqrt(variance + 1e-05) * gain + shift


def edge_update(m, edges, refs):
    edge, pre, table, gather, scatter, w2, eg, eb, count, split = refs
    halves = pre.shape[0]
    for c in range(edges // CHUNK):
        rows = slice(c * CHUNK, (c + 1) * CHUNK)
        hidden = jnp.concatenate(
            [silu(pre[h, m, rows, :] + dot(gather[rows, split:], table[h, m, split:, :])) for h in range(halves)], -1
        )
        out = jnp.concatenate([dot(hidden, w2[h]) for h in range(halves)], -1)
        update = norm(out, eg, eb)
        live = lax.broadcasted_iota(jnp.int32, (CHUNK, 1), 0) + c * CHUNK < count
        edge[m, rows, :] = jnp.where(live, edge[m, rows, :].astype(F32) + update, 0.0).astype(BF16)
    return dot(scatter[...], edge[m]).astype(BF16)


def node_update(m, summed, refs):
    node, node_pre, w3, w4, ng, nb = refs
    halves, half = w4.shape[0], w4.shape[2]
    width = half * halves
    hidden = jnp.concatenate(
        [silu(node_pre[h, m] + dot(summed, w3[h, width:, :])) for h in range(halves)], -1
    )
    out = jnp.concatenate([dot(hidden, w4[h]) for h in range(halves)], -1)
    node[m] = (node[m].astype(F32) + norm(out, ng, nb)).astype(BF16)


def exchange_kernel(
    sizes,
    node_in, edge_in, senders_in, receivers_in, counts_in, halo_in, long_in,
    ef_in, es_in, nf_in, ns_in, eg_in, eb_in, ng_in, nb_in,
    node, edge, pre, node_pre, table, gather, scatter, w2, w3, w4, eg, eb, ng, nb, count_row,
    w1, senders_v, receivers_v, count_s, halo_v, long_v, picked, picker, near, far_rows,
    halo_out, halo, far_out, far,
    local_sem, wl_sem, ws_sem, wr_sem, hs_sem, hr_sem, fs_sem, fr_sem,
):
    n, layers, members, nodes, edges, width, side_rows, slots = sizes
    me = lax.axis_index("dom")
    core = lax.axis_index("mem")
    halves = 2
    other = 1 - core
    split = 2 * nodes

    barrier = pltpu.get_barrier_semaphore()
    pl.semaphore_signal(barrier, inc=1, device_id={"mem": other})
    for step in range(1, n):
        pl.semaphore_signal(barrier, inc=1, device_id={"dom": lax.rem(me + step, n)})

    loads = []
    for place, (src, dst) in enumerate((
        (node_in, node), (halo_in, halo_v), (long_in.at[me], long_v), (senders_in, senders_v),
        (receivers_in, receivers_v), (counts_in, count_s), (edge_in, edge),
        (eg_in, eg), (eb_in, eb), (ng_in, ng), (nb_in, nb),
    )):
        copy = pltpu.make_async_copy(src, dst, local_sem.at[place])
        loads.append(copy)
    weights = ((ef_in, w1), (es_in, w2), (nf_in, w3), (ns_in, w4))
    own = {}
    for l in range(layers):
        for k, (src, dst) in enumerate(weights):
            own[l, k] = pltpu.make_async_copy(src.at[l], dst.at[l, core], wl_sem.at[l, k])
    for copy in loads[:6]:
        copy.start()
    own[0, 0].start()
    loads[6].start()
    for place in loads[7:]:
        place.start()
    for key in own:
        if key != (0, 0):
            own[key].start()

    def column(row):
        wide = round_up(row.shape[1], LANES)
        if wide > row.shape[1]:
            row = jnp.concatenate([row, jnp.zeros((1, wide - row.shape[1]), jnp.int32)], 1)
        return jnp.transpose(jnp.broadcast_to(row, (LANES, wide)))

    def one_hot(hits):
        return hits.astype(F32).astype(BF16)

    loads[1].wait()
    loads[2].wait()
    picked[: 2 * side_rows, :] = column(halo_v[...].reshape(1, 2 * side_rows))[: 2 * side_rows]
    for s in range(slots):
        picked[pl.ds(2 * side_rows + s, n, stride=slots), :] = column(long_v[s : s + 1, :])[:n]
    for c in range(nodes // LANES):
        lane = lax.broadcasted_iota(jnp.int32, picked.shape, 1) + c * LANES
        picker[:, c * LANES : (c + 1) * LANES] = one_hot(picked[...] == lane)

    pending = []
    arrivals = {}

    def send(l, m):
        packed = dot(picker[...], node[m])
        for side in range(2):
            halo_out[l, m, side] = packed[side * side_rows : (side + 1) * side_rows].astype(BF16)
        for q in range(n):
            start = 2 * side_rows + q * slots
            far_out[l, m, q] = packed[start : start + slots].astype(BF16)
        if l == 0 and m == 0:
            pl.semaphore_wait(barrier, n)
        copies = []
        for step in range(1, n):
            target = lax.rem(me + step, n)
            copies.append(pltpu.make_async_remote_copy(
                src_ref=far_out.at[l, m, target],
                dst_ref=far.at[l, m, me],
                send_sem=fs_sem.at[l, m, step],
                recv_sem=fr_sem.at[l, m, step],
                device_id={"dom": target},
            ))
        for side, step in ((1, 1), (0, n - 1)):
            copies.append(pltpu.make_async_remote_copy(
                src_ref=halo_out.at[l, m, side],
                dst_ref=halo.at[l, m, 1 - side],
                send_sem=hs_sem.at[l, m, side],
                recv_sem=hr_sem.at[l, m, side],
                device_id={"dom": lax.rem(me + step, n)},
            ))
        for copy in copies:
            copy.start()
        mine = pltpu.make_async_copy(far_out.at[l, m, me], far.at[l, m, me], fr_sem.at[l, m, 0])
        mine.start()
        pending.extend(copies)
        arrivals[l, m] = (copies, mine)

    def prepare(l, h, ms):
        for m in ms:
            table[h, m, :nodes, :] = dot(node[m], w1[l, h, width : 2 * width, :]).astype(BF16)
            table[h, m, nodes:split, :] = dot(node[m], w1[l, h, 2 * width :, :]).astype(BF16)
        for m in ms:
            pre[h, m] = dot(edge[m], w1[l, h, :width, :]) + dot(gather[:, :split], table[h, m, :split, :])

    def node_prepare(l, m):
        for h in range(halves):
            node_pre[h, m] = dot(node[m], w3[l, h, :width, :])

    def receive(l, m):
        copies, mine = arrivals[l, m]
        for copy in copies:
            copy.wait_recv()
        mine.wait()
        for side in range(2):
            near[m, side * side_rows : (side + 1) * side_rows, :] = halo[l, m, side]
        for q in range(n):
            far_rows[m, q * slots : (q + 1) * slots, :] = far[l, m, q].astype(F32)
        near[m, 2 * side_rows :, :] = far_rows[m].astype(BF16)
        count_near = near.shape[1]
        for h in range(halves):
            table[h, m, split : split + count_near, :] = dot(near[m], w1[l, h, width : 2 * width, :]).astype(BF16)

    loads[0].wait()
    for m in range(members):
        send(0, m)
    partner = {}
    for l in range(layers):
        for k, (src, dst) in enumerate(weights):
            copy = pltpu.make_async_remote_copy(
                src_ref=src.at[l],
                dst_ref=dst.at[l, core],
                send_sem=ws_sem.at[l, k],
                recv_sem=wr_sem.at[l, k],
                device_id={"mem": other},
            )
            copy.start()
            partner[l, k] = copy
            pending.append(copy)

    loads[3].wait()
    loads[4].wait()
    depth = gather.shape[1]
    senders = column(senders_v[...].reshape(1, edges))
    receiver_row = receivers_v[...].reshape(1, edges)
    receivers = column(receiver_row) + nodes
    senders = jnp.where(senders < nodes, senders, senders + nodes)
    for c in range(depth // LANES):
        lane = lax.broadcasted_iota(jnp.int32, (edges, LANES), 1) + c * LANES
        gather[:, c * LANES : (c + 1) * LANES] = one_hot((senders == lane) | (receivers == lane))
    row = lax.broadcasted_iota(jnp.int32, (nodes, edges), 0)
    scatter[...] = one_hot(jnp.broadcast_to(receiver_row, (nodes, edges)) == row)
    far_base = split + near.shape[1]
    if far_base < depth:
        for h in range(halves):
            for m in range(members):
                table[h, m, far_base:, :] = jnp.zeros((depth - far_base, table.shape[3]), BF16)
    loads[5].wait()
    count_row[...] = jnp.full(count_row.shape, count_s[0], jnp.int32)
    for copy in loads[6:]:
        copy.wait()
    own[0, 0].wait()
    everyone = range(members)
    prepare(0, core, everyone)
    partner[0, 0].wait_recv()
    prepare(0, other, everyone)
    for k in (1, 2, 3):
        own[0, k].wait()
        partner[0, k].wait_recv()
    for m in everyone:
        node_prepare(0, m)

    for l in range(layers):
        if l > 0:
            own[l, 0].wait()
            partner[l, 0].wait_recv()
            for h in range(halves):
                prepare(l, h, everyone)
            for k in (1, 2, 3):
                own[l, k].wait()
                partner[l, k].wait_recv()
            for m in everyone:
                node_prepare(l, m)
        for m in everyone:
            receive(l, m)
            if l == layers - 1 and m == members - 1:
                continue
            summed = edge_update(m, edges, (
                edge, pre, table, gather, scatter, w2.at[l], eg[l : l + 1, :], eb[l : l + 1, :],
                count_row[0:1, 0:1], split,
            ))
            node_update(m, summed, (node, node_pre, w3.at[l], w4.at[l], ng[l : l + 1, :], nb[l : l + 1, :]))
            if l < layers - 1:
                send(l + 1, m)
    for copy in pending:
        copy.wait_send()


def finish_kernel(
    sizes,
    node, edge, pre, node_pre, table, gather, scatter, w2, w3, w4, eg, eb, ng, nb, count_row,
    node_out, edge_out, edge_new, node_new, sem,
):
    n, layers, members, nodes, edges, width, side_rows, slots = sizes
    l, m = layers - 1, members - 1
    copies = []

    def store(src, dst):
        copy = pltpu.make_async_copy(src, dst, sem.at[len(copies)])
        copy.start()
        copies.append(copy)

    store(edge.at[:m], edge_out.at[:m])
    store(node.at[:m], node_out.at[:m])
    halves = pre.shape[0]
    split = 2 * nodes
    total = None
    count = count_row[0:1, 0:1]
    for c in range(edges // CHUNK):
        rows = slice(c * CHUNK, (c + 1) * CHUNK)
        hidden = jnp.concatenate(
            [silu(pre[h, m, rows, :] + dot(gather[rows, split:], table[h, m, split:, :])) for h in range(halves)], -1
        )
        out = jnp.concatenate([dot(hidden, w2[l, h]) for h in range(halves)], -1)
        update = norm(out, eg[l : l + 1, :], eb[l : l + 1, :])
        live = lax.broadcasted_iota(jnp.int32, (CHUNK, 1), 0) + c * CHUNK < count
        edge_new[rows, :] = jnp.where(live, edge[m, rows, :].astype(F32) + update, 0.0).astype(BF16)
        store(edge_new.at[rows], edge_out.at[m, rows])
    summed = dot(scatter[...], edge_new[...]).astype(BF16)
    hidden = jnp.concatenate(
        [silu(node_pre[h, m] + dot(summed, w3[l, h, width:, :])) for h in range(halves)], -1
    )
    out = jnp.concatenate([dot(hidden, w4[l, h]) for h in range(halves)], -1)
    update = norm(out, ng[l : l + 1, :], nb[l : l + 1, :])
    node_new[...] = (node[m].astype(F32) + update).astype(BF16)
    store(node_new, node_out.at[m])
    for copy in copies:
        copy.wait()


def solution(mesh):
    n = mesh.shape["dom"]

    def step(
        node, edge, senders, receivers, counts, halo_send, long_send, ef, es, nf, ns, eg, eb, ng, nb
    ):
        members, nodes, width = node.shape
        edges = edge.shape[1]
        layers = ef.shape[0]
        side_rows = halo_send.shape[0] // 2
        slots = long_send.shape[-1]
        long_rows = jnp.swapaxes(long_send, 1, 2)
        near_rows = 2 * side_rows + n * slots
        depth = 2 * nodes + round_up(near_rows, LANES)
        sizes = (n, layers, members, nodes, edges, width, side_rows, slots)
        half = width // 2
        hbm = pl.BlockSpec(memory_space=pltpu.HBM)
        vmem = pl.BlockSpec(memory_space=pltpu.VMEM)
        dma = pltpu.SemaphoreType.DMA
        kept = [
            (node.shape, BF16),
            (edge.shape, BF16),
            ((2, members, edges, half), F32),
            ((2, members, nodes, half), F32),
            ((2, members, depth, half), BF16),
            ((edges, depth), BF16),
            ((nodes, edges), BF16),
            ((layers, 2, es.shape[1], half), BF16),
            ((layers, 2, nf.shape[1], half), BF16),
            ((layers, 2, ns.shape[1], half), BF16),
            (eg.shape, F32),
            (eb.shape, F32),
            (ng.shape, F32),
            (nb.shape, F32),
            ((1, LANES), jnp.int32),
        ]
        state = pl.pallas_call(
            functools.partial(exchange_kernel, sizes),
            out_shape=tuple(pltpu.VMEM(shape, kind) for shape, kind in kept),
            in_specs=[hbm] * 15,
            out_specs=(vmem,) * len(kept),
            scratch_shapes=[
                pltpu.VMEM((layers, 2, ef.shape[1], half), BF16),
                pltpu.VMEM(senders.shape, jnp.int32),
                pltpu.VMEM(receivers.shape, jnp.int32),
                pltpu.SMEM(counts.shape, jnp.int32),
                pltpu.VMEM(halo_send.shape, jnp.int32),
                pltpu.VMEM(long_rows.shape[1:], jnp.int32),
                pltpu.VMEM((near_rows, LANES), jnp.int32),
                pltpu.VMEM((near_rows, nodes), BF16),
                pltpu.VMEM((members, near_rows, width), BF16),
                pltpu.VMEM((members, n * slots, width), F32),
                pltpu.VMEM((layers, members, 2, side_rows, width), BF16),
                pltpu.VMEM((layers, members, 2, side_rows, width), BF16),
                pltpu.VMEM((layers, members, n, slots, width), BF16),
                pltpu.VMEM((layers, members, n, slots, width), BF16),
                dma((11,)),
                dma((layers, 4)),
                dma((layers, 4)),
                dma((layers, 4)),
                dma((layers, members, 2)),
                dma((layers, members, 2)),
                dma((layers, members, n)),
                dma((layers, members, n)),
            ],
            compiler_params=pltpu.CompilerParams(
                collective_id=0, has_side_effects=True, vmem_limit_bytes=51 * 1024 * 1024
            ),
        )(node, edge, senders, receivers, counts, halo_send, long_rows, ef, es, nf, ns, eg, eb, ng, nb)
        return pl.pallas_call(
            functools.partial(finish_kernel, sizes),
            out_shape=(
                jax.ShapeDtypeStruct(node.shape, BF16),
                jax.ShapeDtypeStruct(edge.shape, BF16),
            ),
            in_specs=[vmem] * len(kept),
            out_specs=(hbm, hbm),
            scratch_shapes=[
                pltpu.VMEM((edges, width), BF16),
                pltpu.VMEM((nodes, width), BF16),
                dma((3 + edges // CHUNK,)),
            ],
            compiler_params=pltpu.CompilerParams(vmem_limit_bytes=40 * 1024 * 1024),
        )(*state)

    placed = (
        P("mem", "dom", None),
        P("mem", "dom", None),
        P("dom"),
        P("dom"),
        P("dom"),
        P("dom"),
        P(),
        P(None, None, "mem"),
        P(None, None, "mem"),
        P(None, None, "mem"),
        P(None, None, "mem"),
        P(),
        P(),
        P(),
        P(),
    )
    return jax.shard_map(
        step,
        mesh=mesh,
        in_specs=placed,
        out_specs=(P("mem", "dom", None), P("mem", "dom", None)),
        check_vma=False,
    )
```

profile of v0, /device:TPU:0, one launch (start us, length us, event | category | flops | bytes accessed | tf_op | source)
XLA Modules:
  0.0 26.8 jit_solution(4181625288004939609)
XLA Ops:
  1.3 23.0 %shard_map.158 = (bf16[2,128,512]{2,1,0:T(8,128)(2,1)S(1)}, bf16[2,512,512]{2,1,0:T(8,128)(2,1)S(1)}, f32[2,2,512,256]{3,2,1,0:T(8,128)S(1)}, f32[2,2,128,256]{3...) custom-call(bf16[2,128,512]{2,1,0:T(8,128)(2,1)} %node_in.1, ...), custom_call_target="tpu_custom_call" | custom-call | tf_op jit(solution)/shard_map/pallas_call | solution.py:338
  24.2 2.5 %shard_map.159 = (bf16[2,128,512]{2,1,0:T(8,128)(2,1)}, bf16[2,512,512]{2,1,0:T(8,128)(2,1)}) custom-call(bf16[2,128,512]{2,1,0:T(8,128)(2,1)S(1)} %get-tuple-element.17.node, bf16[2,512,512]{2,1,0:T(8,128)(2,1)S(1)} %get-tuple-element.18.edge, f32[2,2,512,256]{3,2,1,0:T(8,128)S(1)} %get-tuple-element.19.pre, ...), custom_call_target="tpu_custom_call" | custom-call | tf_op jit(solution)/shard_map/pallas_call | solution.py:371
where the time goes:
time: 26.9 us; the launch traced here: 26.8 us
  Pallas kernels  25.5 us (95%)
  between operations  1.29 us (5%)
    pallas_call x1, Pallas kernels, step(): pl.pallas_call(functools.partial(exchange_kernel, sizes), out_shape=tuple...  23 us
    pallas_call x1, Pallas kernels, step(): pl.pallas_call(functools.partial(finish_kernel, sizes), out_shape=(jax.Sh...  2.53 us

commit v1 on v0

v1 whole, which is shorter than its diff:
```python
import functools

import jax
import jax.numpy as jnp
from jax import lax
from jax.experimental import pallas as pl
from jax.experimental.pallas import tpu as pltpu
from jax.sharding import PartitionSpec as P

F32, BF16 = jnp.float32, jnp.bfloat16
LANES = 128
CHUNK = 256


def round_up(value, step):
    return (value + step - 1) // step * step


def dot(a, b):
    return jnp.dot(a, b, preferred_element_type=F32)


def silu_of_half(half):
    return (half + half * jnp.tanh(half)).astype(BF16)


def norm(x, gain, shift):
    average = jnp.mean(x, -1, keepdims=True)
    centred = x - average
    variance = jnp.mean(centred * centred, -1, keepdims=True)
    return centred * lax.rsqrt(variance + 1e-05) * gain + shift


def wide_dot(x, w):
    return jnp.concatenate([dot(x, w[h]) for h in range(w.shape[0])], -1)


def edge_rows(m, c, refs):
    edge, pre, table, gather, w2, eg, eb, count, split = refs
    rows = slice(c * CHUNK, (c + 1) * CHUNK)
    hidden = jnp.concatenate(
        [silu_of_half(pre[h, m, rows, :] + dot(gather[rows, split:], table[h, m, split:, :])) for h in range(2)], -1
    )
    update = norm(wide_dot(hidden, w2), eg, eb)
    live = lax.broadcasted_iota(jnp.int32, (CHUNK, 1), 0) + c * CHUNK < count
    return rows, jnp.where(live, edge[m, rows, :].astype(F32) + update, 0.0).astype(BF16)


def node_rows(base, pre, summed, refs):
    w3b, w4, ng, nb = refs
    hidden = jnp.concatenate([silu_of_half(pre[h] + 0.5 * dot(summed, w3b[h])) for h in range(2)], -1)
    return (base.astype(F32) + norm(wide_dot(hidden, w4), ng, nb)).astype(BF16)


def exchange_kernel(
    sizes,
    node_in, edge_in, senders_in, receivers_in, counts_in, halo_in, long_in,
    ef_in, es_in, nf_in, ns_in, eg_in, eb_in, ng_in, nb_in,
    node, edge, pre, node_pre, table, gather, scatter, weights, norms, count_row,
    ids_v, count_s, halo_v, long_v, picked, picker, sent_scatter, sent, sent_pre, near, far_rows,
    halo_out, halo, far_out, far,
    node_sem, halo_sem, long_sem, ids_sem, count_sem, edge_sem, norm_sem,
    own_sem, ws_sem, wr_sem, hs_sem, hr_sem, fs_sem, fr_sem,
):
    n, layers, members, nodes, edges, width, side_rows, slots = sizes
    me = lax.axis_index("dom")
    core = lax.axis_index("mem")
    halves = 2
    other = 1 - core
    split = 2 * nodes
    near_rows = 2 * side_rows + n * slots
    everyone = range(members)

    barrier = pltpu.get_barrier_semaphore()
    pl.semaphore_signal(barrier, inc=1, device_id={"mem": other})
    for step in range(1, n):
        pl.semaphore_signal(barrier, inc=1, device_id={"dom": lax.rem(me + step, n)})

    def whole(ref, sem):
        return pltpu.make_async_copy(ref, ref, sem)

    blocks = ((ef_in, 0, 3), (es_in, 3, 1), (nf_in, 4, 2), (ns_in, 6, 1))

    def place(l, k, part):
        src, start, count = blocks[k]
        return src.at[l], weights.at[l, part, start * width : (start + count) * width]

    pltpu.make_async_copy(halo_in, halo_v, halo_sem).start()
    pltpu.make_async_copy(long_in.at[me], long_v, long_sem).start()
    pltpu.make_async_copy(node_in, node, node_sem).start()
    pltpu.make_async_copy(senders_in, ids_v.at[0], ids_sem).start()
    pltpu.make_async_copy(receivers_in, ids_v.at[1], ids_sem).start()
    pltpu.make_async_copy(counts_in, count_s, count_sem).start()
    pltpu.make_async_copy(*place(0, 0, core), own_sem.at[0, 0]).start()
    pltpu.make_async_copy(edge_in, edge, edge_sem).start()
    for k, src in enumerate((eg_in, eb_in, ng_in, nb_in)):
        pltpu.make_async_copy(src, norms.at[k], norm_sem).start()
    for l in range(layers):
        for k in range(4):
            if (l, k) != (0, 0):
                pltpu.make_async_copy(*place(l, k, core), own_sem.at[l, min(k, 1)]).start()

    def wait_weights(l, group):
        rows = weights.at[l, core, : 3 * width] if group == 0 else weights.at[l, core, 3 * width :]
        whole(rows, own_sem.at[l, group]).wait()

    def wait_partner(l, group):
        rows = weights.at[l, other, : 3 * width] if group == 0 else weights.at[l, other, 3 * width :]
        whole(rows, wr_sem.at[l, group]).wait()

    def column(row):
        wide = round_up(row.shape[1], LANES)
        if wide > row.shape[1]:
            row = jnp.concatenate([row, jnp.zeros((1, wide - row.shape[1]), jnp.int32)], 1)
        return jnp.transpose(jnp.broadcast_to(row, (LANES, wide)))

    def one_hot(hits):
        return hits.astype(F32).astype(BF16)

    whole(halo_v, halo_sem).wait()
    whole(long_v, long_sem).wait()
    picked[: 2 * side_rows, :] = column(halo_v[...].reshape(1, 2 * side_rows))[: 2 * side_rows]
    for s in range(slots):
        picked[pl.ds(2 * side_rows + s, n, stride=slots), :] = column(long_v[s : s + 1, :])[:n]
    for c in range(nodes // LANES):
        lane = lax.broadcasted_iota(jnp.int32, picked.shape, 1) + c * LANES
        picker[:, c * LANES : (c + 1) * LANES] = one_hot(picked[...] == lane)

    def stage(l, m, packed):
        for side in range(2):
            halo_out[l, m, side] = packed[side * side_rows : (side + 1) * side_rows]
        for q in range(n):
            start = 2 * side_rows + q * slots
            far_out[l, m, q] = packed[start : start + slots]

    def send(l, m):
        for step in range(1, n):
            target = lax.rem(me + step, n)
            pltpu.make_async_remote_copy(
                src_ref=far_out.at[l, m, target],
                dst_ref=far.at[l, m, me],
                send_sem=fs_sem.at[l, m],
                recv_sem=fr_sem.at[l, m],
                device_id={"dom": target},
            ).start()
        for side, step in ((1, 1), (0, n - 1)):
            pltpu.make_async_remote_copy(
                src_ref=halo_out.at[l, m, side],
                dst_ref=halo.at[l, m, 1 - side],
                send_sem=hs_sem.at[l, m],
                recv_sem=hr_sem.at[l, m],
                device_id={"dom": lax.rem(me + step, n)},
            ).start()
        pltpu.make_async_copy(far_out.at[l, m, me], far.at[l, m, me], fr_sem.at[l, m]).start()

    whole(node, node_sem).wait()
    for m in everyone:
        rows = dot(picker[...], node[m]).astype(BF16)
        sent[m] = rows
        stage(0, m, rows)
        if m == 0:
            pl.semaphore_wait(barrier, n)
        send(0, m)
    for l in range(layers):
        for k in range(4):
            src, dst = place(l, k, core)
            pltpu.make_async_remote_copy(
                src_ref=src,
                dst_ref=dst,
                send_sem=ws_sem.at[l],
                recv_sem=wr_sem.at[l, min(k, 1)],
                device_id={"mem": other},
            ).start()

    whole(ids_v, ids_sem).wait()
    depth = gather.shape[1]
    senders = column(ids_v[0:1, :])
    receiver_row = ids_v[1:2, :]
    receivers = column(receiver_row) + nodes
    senders = jnp.where(senders < nodes, senders, senders + nodes)
    for c in range(depth // LANES):
        lane = lax.broadcasted_iota(jnp.int32, (edges, LANES), 1) + c * LANES
        gather[:, c * LANES : (c + 1) * LANES] = one_hot((senders == lane) | (receivers == lane))
    row = lax.broadcasted_iota(jnp.int32, (nodes, edges), 0)
    scatter[...] = one_hot(jnp.broadcast_to(receiver_row, (nodes, edges)) == row)
    sent_scatter[...] = dot(picker[...], scatter[...]).astype(BF16)
    far_base = split + near_rows
    if far_base < depth:
        for h in range(halves):
            for m in everyone:
                table[h, m, far_base:, :] = jnp.zeros((depth - far_base, table.shape[3]), BF16)
    pltpu.make_async_copy(counts_in, count_s, count_sem).wait()
    count_row[...] = jnp.full(count_row.shape, count_s[0], jnp.int32)
    whole(edge, edge_sem).wait()
    whole(norms, norm_sem).wait()

    def prepare(l, h):
        w1 = weights.at[l, h]
        for m in everyone:
            table[h, m, :nodes, :] = (0.5 * dot(node[m], w1[width : 2 * width, :])).astype(BF16)
            table[h, m, nodes:split, :] = (0.5 * dot(node[m], w1[2 * width : 3 * width, :])).astype(BF16)
        for m in everyone:
            pre[h, m] = 0.5 * dot(edge[m], w1[:width, :]) + dot(gather[:, :split], table[h, m, :split, :])

    def node_prepare(l):
        for h in range(halves):
            w3a = weights[l, h, 4 * width : 5 * width, :]
            for m in everyone:
                if l < layers - 1:
                    sent_pre[m, h] = 0.5 * dot(sent[m], w3a)
                node_pre[m, h] = 0.5 * dot(node[m], w3a)

    def receive(l, ms):
        for m in ms:
            whole(far.at[l, m], fr_sem.at[l, m]).wait()
            whole(halo.at[l, m], hr_sem.at[l, m]).wait()
        for m in ms:
            for side in range(2):
                near[m, side * side_rows : (side + 1) * side_rows, :] = halo[l, m, side]
            for q in range(n):
                far_rows[m, q * slots : (q + 1) * slots, :] = far[l, m, q].astype(F32)
            near[m, 2 * side_rows :, :] = far_rows[m].astype(BF16)
            for h in range(halves):
                table[h, m, split : split + near_rows, :] = (
                    0.5 * dot(near[m], weights[l, h, width : 2 * width, :])
                ).astype(BF16)

    wait_weights(0, 0)
    prepare(0, core)
    wait_partner(0, 0)
    prepare(0, other)
    wait_weights(0, 1)
    wait_partner(0, 1)
    node_prepare(0)

    for l in range(layers):
        w = weights.at[l]
        receive(l, everyone)
        if l == layers - 1:
            continue
        node_refs = (
            w.at[:, 5 * width : 6 * width], w.at[:, 6 * width : 7 * width],
            norms[2, l : l + 1, :], norms[3, l : l + 1, :],
        )
        edge_refs = (
            edge, pre, table, gather, w.at[:, 3 * width : 4 * width],
            norms[0, l : l + 1, :], norms[1, l : l + 1, :], count_row[0:1, 0:1], split,
        )
        for c in range(edges // CHUNK):
            for m in everyone:
                rows, value = edge_rows(m, c, edge_refs)
                edge[m, rows, :] = value
        summed = jnp.concatenate([dot(sent_scatter[...], edge[m]).astype(BF16) for m in everyone], 0)
        base = jnp.concatenate([sent[m] for m in everyone], 0)
        started = [jnp.concatenate([sent_pre[m, h] for m in everyone], 0) for h in range(halves)]
        fresh = node_rows(base, started, summed, node_refs)
        for m in everyone:
            rows = fresh[m * near_rows : (m + 1) * near_rows]
            if l + 1 < layers - 1:
                sent[m] = rows
            stage(l + 1, m, rows)
            send(l + 1, m)
        for m in everyone:
            summed = dot(scatter[...], edge[m]).astype(BF16)
            node[m] = node_rows(node[m], [node_pre[m, h] for h in range(halves)], summed, node_refs)
        wait_weights(l + 1, 0)
        wait_partner(l + 1, 0)
        for h in range(halves):
            prepare(l + 1, h)
        wait_weights(l + 1, 1)
        wait_partner(l + 1, 1)
        node_prepare(l + 1)

    for l in range(layers):
        whole(weights.at[l, core], ws_sem.at[l]).wait()
        for m in everyone:
            whole(far_out.at[l, m, : n - 1], fs_sem.at[l, m]).wait()
            whole(halo_out.at[l, m], hs_sem.at[l, m]).wait()


def finish_kernel(
    sizes,
    node, edge, pre, node_pre, table, gather, scatter, weights, norms, count_row,
    node_out, edge_out, edge_new, node_new, sem,
):
    n, layers, members, nodes, edges, width, side_rows, slots = sizes
    l = layers - 1
    w = weights.at[l]
    copies = []

    def store(src, dst):
        copy = pltpu.make_async_copy(src, dst, sem.at[len(copies)])
        copy.start()
        copies.append(copy)

    everyone = range(members)
    halves = 2
    edge_refs = (
        edge, pre, table, gather, w.at[:, 3 * width : 4 * width],
        norms[0, l : l + 1, :], norms[1, l : l + 1, :], count_row[0:1, 0:1], 2 * nodes,
    )
    node_refs = (
        w.at[:, 5 * width : 6 * width], w.at[:, 6 * width : 7 * width],
        norms[2, l : l + 1, :], norms[3, l : l + 1, :],
    )
    for c in range(edges // CHUNK):
        for m in everyone:
            rows, value = edge_rows(m, c, edge_refs)
            edge_new[m, rows, :] = value
            store(edge_new.at[m, rows], edge_out.at[m, rows])
    summed = jnp.concatenate([dot(scatter[...], edge_new[m]).astype(BF16) for m in everyone], 0)
    base = jnp.concatenate([node[m] for m in everyone], 0)
    started = [jnp.concatenate([node_pre[m, h] for m in everyone], 0) for h in range(halves)]
    fresh = node_rows(base, started, summed, node_refs)
    for m in everyone:
        node_new[m] = fresh[m * nodes : (m + 1) * nodes]
    store(node_new, node_out)
    for copy in copies:
        copy.wait()


def solution(mesh):
    n = mesh.shape["dom"]

    def step(
        node, edge, senders, receivers, counts, halo_send, long_send, ef, es, nf, ns, eg, eb, ng, nb
    ):
        members, nodes, width = node.shape
        edges = edge.shape[1]
        layers = ef.shape[0]
        side_rows = halo_send.shape[0] // 2
        slots = long_send.shape[-1]
        long_rows = jnp.swapaxes(long_send, 1, 2)
        near_rows = 2 * side_rows + n * slots
        depth = 2 * nodes + round_up(near_rows, LANES)
        sizes = (n, layers, members, nodes, edges, width, side_rows, slots)
        half = width // 2
        hbm = pl.BlockSpec(memory_space=pltpu.HBM)
        vmem = pl.BlockSpec(memory_space=pltpu.VMEM)
        dma = pltpu.SemaphoreType.DMA
        kept = [
            (node.shape, BF16),
            (edge.shape, BF16),
            ((2, members, edges, half), F32),
            ((members, 2, nodes, half), F32),
            ((2, members, depth, half), BF16),
            ((edges, depth), BF16),
            ((nodes, edges), BF16),
            ((layers, 2, 7 * width, half), BF16),
            ((4,) + eg.shape, F32),
            ((1, LANES), jnp.int32),
        ]
        state = pl.pallas_call(
            functools.partial(exchange_kernel, sizes),
            out_shape=tuple(pltpu.VMEM(shape, kind) for shape, kind in kept),
            in_specs=[hbm] * 15,
            out_specs=(vmem,) * len(kept),
            scratch_shapes=[
                pltpu.VMEM((2,) + senders.shape, jnp.int32),
                pltpu.SMEM(counts.shape, jnp.int32),
                pltpu.VMEM(halo_send.shape, jnp.int32),
                pltpu.VMEM(long_rows.shape[1:], jnp.int32),
                pltpu.VMEM((near_rows, LANES), jnp.int32),
                pltpu.VMEM((near_rows, nodes), BF16),
                pltpu.VMEM((near_rows, edges), BF16),
                pltpu.VMEM((members, near_rows, width), BF16),
                pltpu.VMEM((members, 2, near_rows, half), F32),
                pltpu.VMEM((members, near_rows, width), BF16),
                pltpu.VMEM((members, n * slots, width), F32),
                pltpu.VMEM((layers, members, 2, side_rows, width), BF16),
                pltpu.VMEM((layers, members, 2, side_rows, width), BF16),
                pltpu.VMEM((layers, members, n, slots, width), BF16),
                pltpu.VMEM((layers, members, n, slots, width), BF16),
            ] + [dma(())] * 7 + [
                dma((layers, 2)),
                dma((layers,)),
                dma((layers, 2)),
                dma((layers, members)),
                dma((layers, members)),
                dma((layers, members)),
                dma((layers, members)),
            ],
            compiler_params=pltpu.CompilerParams(
                collective_id=0, has_side_effects=True, vmem_limit_bytes=51 * 1024 * 1024
            ),
        )(node, edge, senders, receivers, counts, halo_send, long_rows, ef, es, nf, ns, eg, eb, ng, nb)
        return pl.pallas_call(
            functools.partial(finish_kernel, sizes),
            out_shape=(
                jax.ShapeDtypeStruct(node.shape, BF16),
                jax.ShapeDtypeStruct(edge.shape, BF16),
            ),
            in_specs=[vmem] * len(kept),
            out_specs=(hbm, hbm),
            scratch_shapes=[
                pltpu.VMEM(edge.shape, BF16),
                pltpu.VMEM(node.shape, BF16),
                dma((1 + members * (edges // CHUNK),)),
            ],
            compiler_params=pltpu.CompilerParams(vmem_limit_bytes=40 * 1024 * 1024),
        )(*state)

    shared, halved = P(), P(None, None, "mem")
    parts = P("mem", "dom", None)
    placed = (parts,) * 2 + (P("dom"),) * 4 + (shared,) + (halved,) * 4 + (shared,) * 4
    return jax.shard_map(step, mesh=mesh, in_specs=placed, out_specs=(parts, parts), check_vma=False)
```

time: 26.9 us -> 31.5 us (1.17)
  local copies, waits for them, and re-layouts: 0 us -> 5.78 us
  Pallas kernels: 25.5 us -> 24.2 us
    unnamed x0 -> x12, local copies, waits for them, and re-layouts: none -> 5.78 us
    pallas_call x1, Pallas kernels: 23 us -> 20.7 us  [step(): pl.pallas_call(functools.partial(exchange_kernel, sizes), out_shape=tuple...]
    pallas_call x1, Pallas kernels: 2.53 us -> 3.48 us  [step(): pl.pallas_call(functools.partial(finish_kernel, sizes), out_shape=(jax.Sh...]
where the time goes in v1:
time: 31.5 us; the launch traced here: 31.3 us
  Pallas kernels  24.2 us (77%)
  local copies, waits for them, and re-layouts  5.78 us (18%)
  between operations  1.3 us (4%)
    pallas_call x1, Pallas kernels, step(): pl.pallas_call(functools.partial(exchange_kernel, sizes), out_shape=tuple...  20.7 us
    unnamed x12, local copies, waits for them, and re-layouts  5.78 us
    pallas_call x1, Pallas kernels, step(): pl.pallas_call(functools.partial(finish_kernel, sizes), out_shape=(jax.Sh...  3.48 us

profile of v1, /device:TPU:0, one launch (start us, length us, event | category | flops | bytes accessed | tf_op | source)
XLA Modules:
  0.0 31.3 jit_solution(16090519142035386926)
XLA Ops:
  1.3 20.7 %shard_map.158 = (bf16[2,128,512]{2,1,0:T(8,128)(2,1)S(1)}, bf16[2,512,512]{2,1,0:T(8,128)(2,1)S(1)}, f32[2,2,512,256]{3,2,1,0:T(8,128)S(1)}, f32[2,2,128,256]{3...) custom-call(bf16[2,128,512]{2,1,0:T(8,128)(2,1)} %node_in.1, ...), custom_call_target="tpu_custom_call" | custom-call | tf_op jit(solution)/shard_map/pallas_call | solution.py:353
  22.0 0.0 copy-start
  22.0 1.0 %copy-done = bf16[2,512,512]{2,1,0:T(8,128)(2,1)} copy-done((bf16[2,512,512]{2,1,0:T(8,128)(2,1)}, bf16[2,512,512]{2,1,0:T(8,128)(2,1)S(1)}, u32[]{:S(2)}) %copy-start) | copy-done | bytes 1048600
  23.0 0.0 copy-start.2
  23.0 0.8 %copy-done.2 = f32[2,2,128,256]{3,2,1,0:T(8,128)} copy-done((f32[2,2,128,256]{3,2,1,0:T(8,128)}, f32[2,2,128,256]{3,2,1,0:T(8,128)S(1)}, u32[]{:S(2)}) %copy-start.2) | copy-done | bytes 524312
  23.8 0.0 copy-start.4
  23.8 0.8 %copy-done.4 = bf16[512,384]{1,0:T(8,128)(2,1)} copy-done((bf16[512,384]{1,0:T(8,128)(2,1)}, bf16[512,384]{1,0:T(8,128)(2,1)S(1)}, u32[]{:S(2)}) %copy-start.4) | copy-done | bytes 393240
  24.5 0.0 copy-start.1
  24.5 1.2 %copy-done.1 = bf16[2,512,512]{2,1,0:T(8,128)(2,1)S(1)} copy-done((bf16[2,512,512]{2,1,0:T(8,128)(2,1)S(1)}, bf16[2,512,512]{2,1,0:T(8,128)(2,1)}, u32[]{:S(2)}) %copy-start.1) | copy-done | bytes 1048600
  25.7 0.0 copy-start.3
  25.7 1.0 %copy-done.3 = f32[2,2,128,256]{3,2,1,0:T(8,128)S(1)} copy-done((f32[2,2,128,256]{3,2,1,0:T(8,128)S(1)}, f32[2,2,128,256]{3,2,1,0:T(8,128)}, u32[]{:S(2)}) %copy-start.3) | copy-done | bytes 524312
  26.8 0.0 copy-start.5
  26.8 1.0 %copy-done.5 = bf16[512,384]{1,0:T(8,128)(2,1)S(1)} copy-done((bf16[512,384]{1,0:T(8,128)(2,1)S(1)}, bf16[512,384]{1,0:T(8,128)(2,1)}, u32[]{:S(2)}) %copy-start.5) | copy-done | bytes 393240
  27.8 3.5 %shard_map.159 = (bf16[2,128,512]{2,1,0:T(8,128)(2,1)}, bf16[2,512,512]{2,1,0:T(8,128)(2,1)}) custom-call(bf16[2,128,512]{2,1,0:T(8,128)(2,1)S(1)} %get-tuple-element.12.node, bf16[2,512,512]{2,1,0:T(8,128)(2,1)S(1)} %copy-done.1, f32[2,2,512,256]{3,2,1,0:T(8,128)S(1)} %get-tuple-element.14.pre, f32[2,2,128,256]{3,2,1,0:T(8,128)S(1)} %copy-done.3, ...), custom_call_target="tpu_custom_call" | custom-call | tf_op jit(solution)/shard_map/pallas_call | solution.py:387
Async XLA Ops:
  22.0 1.0 %copy-start = (bf16[2,512,512]{2,1,0:T(8,128)(2,1)}, bf16[2,512,512]{2,1,0:T(8,128)(2,1)S(1)}, u32[]{:S(2)}) copy-start(bf16[2,512,512]{2,1,0:T(8,128)(2,1)S(1)} %get-tuple-element.13.edge) | copy-start | bytes 3145732
  23.0 0.8 %copy-start.2 = (f32[2,2,128,256]{3,2,1,0:T(8,128)}, f32[2,2,128,256]{3,2,1,0:T(8,128)S(1)}, u32[]{:S(2)}) copy-start(f32[2,2,128,256]{3,2,1,0:T(8,128)S(1)} %get-tuple-element.15.node_pre) | copy-start | bytes 1572868
  23.8 0.8 %copy-start.4 = (bf16[512,384]{1,0:T(8,128)(2,1)}, bf16[512,384]{1,0:T(8,128)(2,1)S(1)}, u32[]{:S(2)}) copy-start(bf16[512,384]{1,0:T(8,128)(2,1)S(1)} %get-tuple-element.17.gather) | copy-start | bytes 1179652
  24.5 1.2 %copy-start.1 = (bf16[2,512,512]{2,1,0:T(8,128)(2,1)S(1)}, bf16[2,512,512]{2,1,0:T(8,128)(2,1)}, u32[]{:S(2)}) copy-start(bf16[2,512,512]{2,1,0:T(8,128)(2,1)} %copy-done) | copy-start | bytes 3145732
  25.7 1.0 %copy-start.3 = (f32[2,2,128,256]{3,2,1,0:T(8,128)S(1)}, f32[2,2,128,256]{3,2,1,0:T(8,128)}, u32[]{:S(2)}) copy-start(f32[2,2,128,256]{3,2,1,0:T(8,128)} %copy-done.2) | copy-start | bytes 1572868
  26.8 1.0 %copy-start.5 = (bf16[512,384]{1,0:T(8,128)(2,1)S(1)}, bf16[512,384]{1,0:T(8,128)(2,1)}, u32[]{:S(2)}) copy-start(bf16[512,384]{1,0:T(8,128)(2,1)} %copy-done.4) | copy-start | bytes 1179652

commit v2 on v1

--- a/solution.py
+++ b/solution.py
@@ -24,40 +24,43 @@
     return (half + half * jnp.tanh(half)).astype(BF16)
 
 
-def norm(x, gain, shift):
-    average = jnp.mean(x, -1, keepdims=True)
-    centred = x - average
-    variance = jnp.mean(centred * centred, -1, keepdims=True)
-    return centred * lax.rsqrt(variance + 1e-05) * gain + shift
-
-
 def wide_dot(x, w):
     return jnp.concatenate([dot(x, w[h]) for h in range(w.shape[0])], -1)
 
 
+def scaled(x, gain, live=None):
+    factor = lax.rsqrt(jnp.mean(x * x, -1, keepdims=True) + 1e-05)
+    if live is not None:
+        factor = jnp.where(live, factor, 0.0)
+    return x * factor * gain
+
+
+def live_rows(start, rows, count):
+    return lax.broadcasted_iota(jnp.int32, (rows, 1), 0) + start < count
+
+
 def edge_rows(m, c, refs):
-    edge, pre, table, gather, w2, eg, eb, count, split = refs
+    base, pre, table, gather, w2, gain, count, split = refs
     rows = slice(c * CHUNK, (c + 1) * CHUNK)
     hidden = jnp.concatenate(
         [silu_of_half(pre[h, m, rows, :] + dot(gather[rows, split:], table[h, m, split:, :])) for h in range(2)], -1
     )
-    update = norm(wide_dot(hidden, w2), eg, eb)
-    live = lax.broadcasted_iota(jnp.int32, (CHUNK, 1), 0) + c * CHUNK < count
-    return rows, jnp.where(live, edge[m, rows, :].astype(F32) + update, 0.0).astype(BF16)
+    update = scaled(wide_dot(hidden, w2), gain, live_rows(c * CHUNK, CHUNK, count))
+    return rows, (base[m, rows, :] + update).astype(BF16)
 
 
 def node_rows(base, pre, summed, refs):
-    w3b, w4, ng, nb = refs
+    w3b, w4, gain = refs
     hidden = jnp.concatenate([silu_of_half(pre[h] + 0.5 * dot(summed, w3b[h])) for h in range(2)], -1)
-    return (base.astype(F32) + norm(wide_dot(hidden, w4), ng, nb)).astype(BF16)
+    return (base + scaled(wide_dot(hidden, w4), gain)).astype(BF16)
 
 
 def exchange_kernel(
     sizes,
     node_in, edge_in, senders_in, receivers_in, counts_in, halo_in, long_in,
     ef_in, es_in, nf_in, ns_in, eg_in, eb_in, ng_in, nb_in,
-    node, edge, pre, node_pre, table, gather, scatter, weights, norms, count_row,
-    ids_v, count_s, halo_v, long_v, picked, picker, sent_scatter, sent, sent_pre, near, far_rows,
+    node_base, edge_base, pre, node_pre, table, gather, scatter, weights, norms, count_row,
+    node, edge, first, ids_v, count_s, halo_v, long_v, picked, picker, sent_scatter, sent, sent_base, sent_pre, near, far_rows,
     halo_out, halo, far_out, far,
     node_sem, halo_sem, long_sem, ids_sem, count_sem, edge_sem, norm_sem,
     own_sem, ws_sem, wr_sem, hs_sem, hr_sem, fs_sem, fr_sem,
@@ -71,6 +74,10 @@
     near_rows = 2 * side_rows + n * slots
     everyone = range(members)
 
+    pltpu.make_async_copy(halo_in, halo_v, halo_sem).start()
+    pltpu.make_async_copy(long_in.at[me], long_v, long_sem).start()
+    pltpu.make_async_copy(node_in, node, node_sem).start()
+
     barrier = pltpu.get_barrier_semaphore()
     pl.semaphore_signal(barrier, inc=1, device_id={"mem": other})
     for step in range(1, n):
@@ -79,15 +86,13 @@
     def whole(ref, sem):
         return pltpu.make_async_copy(ref, ref, sem)
 
-    blocks = ((ef_in, 0, 3), (es_in, 3, 1), (nf_in, 4, 2), (ns_in, 6, 1))
+    blocks = ((ef_in, 0, 3), (es_in, 0, 1), (nf_in, 1, 2), (ns_in, 3, 1))
 
     def place(l, k, part):
         src, start, count = blocks[k]
-        return src.at[l], weights.at[l, part, start * width : (start + count) * width]
-
-    pltpu.make_async_copy(halo_in, halo_v, halo_sem).start()
-    pltpu.make_async_copy(long_in.at[me], long_v, long_sem).start()
-    pltpu.make_async_copy(node_in, node, node_sem).start()
+        held = weights if k else first
+        return src.at[l], held.at[l, part, start * width : (start + count) * width]
+
     pltpu.make_async_copy(senders_in, ids_v.at[0], ids_sem).start()
     pltpu.make_async_copy(receivers_in, ids_v.at[1], ids_sem).start()
     pltpu.make_async_copy(counts_in, count_s, count_sem).start()
@@ -101,12 +106,10 @@
                 pltpu.make_async_copy(*place(l, k, core), own_sem.at[l, min(k, 1)]).start()
 
     def wait_weights(l, group):
-        rows = weights.at[l, core, : 3 * width] if group == 0 else weights.at[l, core, 3 * width :]
-        whole(rows, own_sem.at[l, group]).wait()
+        whole((weights if group else first).at[l, core], own_sem.at[l, group]).wait()
 
     def wait_partner(l, group):
-        rows = weights.at[l, other, : 3 * width] if group == 0 else weights.at[l, other, 3 * width :]
-        whole(rows, wr_sem.at[l, group]).wait()
+        whole((weights if group else first).at[l, other], wr_sem.at[l, group]).wait()
 
     def column(row):
         wide = round_up(row.shape[1], LANES)
@@ -128,46 +131,45 @@
 
     def stage(l, m, packed):
         for side in range(2):
-            halo_out[l, m, side] = packed[side * side_rows : (side + 1) * side_rows]
+            halo_out[l, side, m] = packed[side * side_rows : (side + 1) * side_rows]
         for q in range(n):
             start = 2 * side_rows + q * slots
-            far_out[l, m, q] = packed[start : start + slots]
-
-    def send(l, m):
+            far_out[l, q, m] = packed[start : start + slots]
+
+    def send(l):
+        for side, step in ((1, 1), (0, n - 1)):
+            pltpu.make_async_remote_copy(
+                src_ref=halo_out.at[l, side],
+                dst_ref=halo.at[l, 1 - side],
+                send_sem=hs_sem.at[l],
+                recv_sem=hr_sem.at[l],
+                device_id={"dom": lax.rem(me + step, n)},
+            ).start()
         for step in range(1, n):
             target = lax.rem(me + step, n)
             pltpu.make_async_remote_copy(
-                src_ref=far_out.at[l, m, target],
-                dst_ref=far.at[l, m, me],
-                send_sem=fs_sem.at[l, m],
-                recv_sem=fr_sem.at[l, m],
+                src_ref=far_out.at[l, target],
+                dst_ref=far.at[l, me],
+                send_sem=fs_sem.at[l],
+                recv_sem=fr_sem.at[l],
                 device_id={"dom": target},
             ).start()
-        for side, step in ((1, 1), (0, n - 1)):
-            pltpu.make_async_remote_copy(
-                src_ref=halo_out.at[l, m, side],
-                dst_ref=halo.at[l, m, 1 - side],
-                send_sem=hs_sem.at[l, m],
-                recv_sem=hr_sem.at[l, m],
-                device_id={"dom": lax.rem(me + step, n)},
-            ).start()
-        pltpu.make_async_copy(far_out.at[l, m, me], far.at[l, m, me], fr_sem.at[l, m]).start()
+        pltpu.make_async_copy(far_out.at[l, me], far.at[l, me], fr_sem.at[l]).start()
 
     whole(node, node_sem).wait()
     for m in everyone:
         rows = dot(picker[...], node[m]).astype(BF16)
         sent[m] = rows
         stage(0, m, rows)
-        if m == 0:
-            pl.semaphore_wait(barrier, n)
-        send(0, m)
+    pl.semaphore_wait(barrier, n)
+    send(0)
     for l in range(layers):
         for k in range(4):
             src, dst = place(l, k, core)
             pltpu.make_async_remote_copy(
                 src_ref=src,
                 dst_ref=dst,
-                send_sem=ws_sem.at[l],
+                send_sem=ws_sem.at[l, min(k, 1)],
                 recv_sem=wr_sem.at[l, min(k, 1)],
                 device_id={"mem": other},
             ).start()
@@ -195,36 +197,57 @@
     whole(norms, norm_sem).wait()
 
     def prepare(l, h):
-        w1 = weights.at[l, h]
+        w1 = first.at[l, h]
         for m in everyone:
             table[h, m, :nodes, :] = (0.5 * dot(node[m], w1[width : 2 * width, :])).astype(BF16)
             table[h, m, nodes:split, :] = (0.5 * dot(node[m], w1[2 * width : 3 * width, :])).astype(BF16)
         for m in everyone:
             pre[h, m] = 0.5 * dot(edge[m], w1[:width, :]) + dot(gather[:, :split], table[h, m, :split, :])
 
+    def centre(l, start):
+        for r in range(start, start + width, LANES):
+            rows = slice(r, r + LANES)
+            values = [weights[l, h, rows, :].astype(F32) for h in range(halves)]
+            average = sum(jnp.sum(v, -1, keepdims=True) for v in values) / width
+            for h in range(halves):
+                weights[l, h, rows, :] = (values[h] - average).astype(BF16)
+
+    def edge_prepare(l):
+        for m in everyone:
+            for r in range(0, edges, LANES):
+                rows = slice(r, r + LANES)
+                live = live_rows(r, LANES, count_row[0:1, 0:1])
+                edge_base[m, rows, :] = jnp.where(live, edge[m, rows, :].astype(F32) + norms[1, l : l + 1, :], 0.0)
+
     def node_prepare(l):
+        centre(l, 0)
+        centre(l, 3 * width)
+        for m in everyone:
+            node_base[m] = node[m].astype(F32) + norms[3, l : l + 1, :]
+            if l < layers - 1:
+                sent_base[m * near_rows : (m + 1) * near_rows, :] = sent[m].astype(F32) + norms[3, l : l + 1, :]
         for h in range(halves):
-            w3a = weights[l, h, 4 * width : 5 * width, :]
+            w3a = weights[l, h, width : 2 * width, :]
             for m in everyone:
                 if l < layers - 1:
                     sent_pre[m, h] = 0.5 * dot(sent[m], w3a)
                 node_pre[m, h] = 0.5 * dot(node[m], w3a)
 
     def receive(l, ms):
-        for m in ms:
-            whole(far.at[l, m], fr_sem.at[l, m]).wait()
-            whole(halo.at[l, m], hr_sem.at[l, m]).wait()
+        whole(far.at[l], fr_sem.at[l]).wait()
+        whole(halo.at[l], hr_sem.at[l]).wait()
         for m in ms:
             for side in range(2):
-                near[m, side * side_rows : (side + 1) * side_rows, :] = halo[l, m, side]
+                near[m, side * side_rows : (side + 1) * side_rows, :] = halo[l, side, m]
             for q in range(n):
-                far_rows[m, q * slots : (q + 1) * slots, :] = far[l, m, q].astype(F32)
+                far_rows[m, q * slots : (q + 1) * slots, :] = far[l, q, m].astype(F32)
             near[m, 2 * side_rows :, :] = far_rows[m].astype(BF16)
             for h in range(halves):
                 table[h, m, split : split + near_rows, :] = (
-                    0.5 * dot(near[m], weights[l, h, width : 2 * width, :])
+                    0.5 * dot(near[m], first[l, h, width : 2 * width, :])
                 ).astype(BF16)
 
+    edge_prepare(0)
     wait_weights(0, 0)
     prepare(0, core)
     wait_partner(0, 0)
@@ -239,30 +262,30 @@
         if l == layers - 1:
             continue
         node_refs = (
-            w.at[:, 5 * width : 6 * width], w.at[:, 6 * width : 7 * width],
-            norms[2, l : l + 1, :], norms[3, l : l + 1, :],
+            w.at[:, 2 * width : 3 * width], w.at[:, 3 * width :],
+            norms[2, l : l + 1, :],
         )
         edge_refs = (
-            edge, pre, table, gather, w.at[:, 3 * width : 4 * width],
-            norms[0, l : l + 1, :], norms[1, l : l + 1, :], count_row[0:1, 0:1], split,
+            edge_base, pre, table, gather, w.at[:, :width],
+            norms[0, l : l + 1, :], count_row[0:1, 0:1], split,
         )
         for c in range(edges // CHUNK):
             for m in everyone:
                 rows, value = edge_rows(m, c, edge_refs)
                 edge[m, rows, :] = value
         summed = jnp.concatenate([dot(sent_scatter[...], edge[m]).astype(BF16) for m in everyone], 0)
-        base = jnp.concatenate([sent[m] for m in everyone], 0)
         started = [jnp.concatenate([sent_pre[m, h] for m in everyone], 0) for h in range(halves)]
-        fresh = node_rows(base, started, summed, node_refs)
+        fresh = node_rows(sent_base[...], started, summed, node_refs)
         for m in everyone:
             rows = fresh[m * near_rows : (m + 1) * near_rows]
             if l + 1 < layers - 1:
                 sent[m] = rows
             stage(l + 1, m, rows)
-            send(l + 1, m)
+        send(l + 1)
         for m in everyone:
             summed = dot(scatter[...], edge[m]).astype(BF16)
-            node[m] = node_rows(node[m], [node_pre[m, h] for h in range(halves)], summed, node_refs)
+            node[m] = node_rows(node_base[m], [node_pre[m, h] for h in range(halves)], summed, node_refs)
+        edge_prepare(l + 1)
         wait_weights(l + 1, 0)
         wait_partner(l + 1, 0)
         for h in range(halves):
@@ -272,15 +295,15 @@
         node_prepare(l + 1)
 
     for l in range(layers):
-        whole(weights.at[l, core], ws_sem.at[l]).wait()
-        for m in everyone:
-            whole(far_out.at[l, m, : n - 1], fs_sem.at[l, m]).wait()
-            whole(halo_out.at[l, m], hs_sem.at[l, m]).wait()
+        whole(first.at[l, core], ws_sem.at[l, 0]).wait()
+        whole(weights.at[l, core], ws_sem.at[l, 1]).wait()
+        whole(far_out.at[l, : n - 1], fs_sem.at[l]).wait()
+        whole(halo_out.at[l], hs_sem.at[l]).wait()
 
 
 def finish_kernel(
     sizes,
-    node, edge, pre, node_pre, table, gather, scatter, weights, norms, count_row,
+    node_base, edge_base, pre, node_pre, table, gather, scatter, weights, norms, count_row,
     node_out, edge_out, edge_new, node_new, sem,
 ):
     n, layers, members, nodes, edges, width, side_rows, slots = sizes
@@ -296,12 +319,12 @@
     everyone = range(members)
     halves = 2
     edge_refs = (
-        edge, pre, table, gather, w.at[:, 3 * width : 4 * width],
-        norms[0, l : l + 1, :], norms[1, l : l + 1, :], count_row[0:1, 0:1], 2 * nodes,
+        edge_base, pre, table, gather, w.at[:, :width],
+        norms[0, l : l + 1, :], count_row[0:1, 0:1], 2 * nodes,
     )
     node_refs = (
-        w.at[:, 5 * width : 6 * width], w.at[:, 6 * width : 7 * width],
-        norms[2, l : l + 1, :], norms[3, l : l + 1, :],
+        w.at[:, 2 * width : 3 * width], w.at[:, 3 * width :],
+        norms[2, l : l + 1, :],
     )
     for c in range(edges // CHUNK):
         for m in everyone:
@@ -309,7 +332,7 @@
             edge_new[m, rows, :] = value
             store(edge_new.at[m, rows], edge_out.at[m, rows])
     summed = jnp.concatenate([dot(scatter[...], edge_new[m]).astype(BF16) for m in everyone], 0)
-    base = jnp.concatenate([node[m] for m in everyone], 0)
+    base = jnp.concatenate([node_base[m] for m in everyone], 0)
     started = [jnp.concatenate([node_pre[m, h] for m in everyone], 0) for h in range(halves)]
     fresh = node_rows(base, started, summed, node_refs)
     for m in everyone:
@@ -339,14 +362,14 @@
         vmem = pl.BlockSpec(memory_space=pltpu.VMEM)
         dma = pltpu.SemaphoreType.DMA
         kept = [
-            (node.shape, BF16),
-            (edge.shape, BF16),
+            (node.shape, F32),
+            (edge.shape, F32),
             ((2, members, edges, half), F32),
             ((members, 2, nodes, half), F32),
             ((2, members, depth, half), BF16),
             ((edges, depth), BF16),
             ((nodes, edges), BF16),
-            ((layers, 2, 7 * width, half), BF16),
+            ((layers, 2, 4 * width, half), BF16),
             ((4,) + eg.shape, F32),
             ((1, LANES), jnp.int32),
         ]
@@ -356,6 +379,9 @@
             in_specs=[hbm] * 15,
             out_specs=(vmem,) * len(kept),
             scratch_shapes=[
+                pltpu.VMEM(node.shape, BF16),
+                pltpu.VMEM(edge.shape, BF16),
+                pltpu.VMEM((layers, 2, ef.shape[1], half), BF16),
                 pltpu.VMEM((2,) + senders.shape, jnp.int32),
                 pltpu.SMEM(counts.shape, jnp.int32),
                 pltpu.VMEM(halo_send.shape, jnp.int32),
@@ -364,21 +390,22 @@
                 pltpu.VMEM((near_rows, nodes), BF16),
                 pltpu.VMEM((near_rows, edges), BF16),
                 pltpu.VMEM((members, near_rows, width), BF16),
+                pltpu.VMEM((members * near_rows, width), F32),
                 pltpu.VMEM((members, 2, near_rows, half), F32),
                 pltpu.VMEM((members, near_rows, width), BF16),
                 pltpu.VMEM((members, n * slots, width), F32),
-                pltpu.VMEM((layers, members, 2, side_rows, width), BF16),
-                pltpu.VMEM((layers, members, 2, side_rows, width), BF16),
-                pltpu.VMEM((layers, members, n, slots, width), BF16),
-                pltpu.VMEM((layers, members, n, slots, width), BF16),
+                pltpu.VMEM((layers, 2, members, side_rows, width), BF16),
+                pltpu.VMEM((layers, 2, members, side_rows, width), BF16),
+                pltpu.VMEM((layers, n, members, slots, width), BF16),
+                pltpu.VMEM((layers, n, members, slots, width), BF16),
             ] + [dma(())] * 7 + [
                 dma((layers, 2)),
+                dma((layers, 2)),
+                dma((layers, 2)),
                 dma((layers,)),
-                dma((layers, 2)),
-                dma((layers, members)),
-                dma((layers, members)),
-                dma((layers, members)),
-                dma((layers, members)),
+                dma((layers,)),
+                dma((layers,)),
+                dma((layers,)),
             ],
             compiler_params=pltpu.CompilerParams(
                 collective_id=0, has_side_effects=True, vmem_limit_bytes=51 * 1024 * 1024

time: 31.5 us -> 24.3 us (0.77)
  local copies, waits for them, and re-layouts: 5.78 us -> 0 us
  Pallas kernels: 24.2 us -> 22.8 us
    unnamed x12 -> x0, local copies, waits for them, and re-layouts: 5.78 us -> none
    pallas_call x1, Pallas kernels: 20.7 us -> 19.8 us  [step(): pl.pallas_call(functools.partial(exchange_kernel, sizes), out_shape=tuple...]
    pallas_call x1, Pallas kernels: 3.48 us -> 2.98 us  [step(): pl.pallas_call(functools.partial(finish_kernel, sizes), out_shape=(jax.Sh...]
where the time goes in v2:
time: 24.3 us; the launch traced here: 24.1 us
  Pallas kernels  22.8 us (94%)
  between operations  1.29 us (5%)
    pallas_call x1, Pallas kernels, step(): pl.pallas_call(functools.partial(exchange_kernel, sizes), out_shape=tuple...  19.8 us
    pallas_call x1, Pallas kernels, step(): pl.pallas_call(functools.partial(finish_kernel, sizes), out_shape=(jax.Sh...  2.98 us

profile of v2, /device:TPU:0, one launch (start us, length us, event | category | flops | bytes accessed | tf_op | source)
XLA Modules:
  0.0 24.1 jit_solution(3675587664694204727)
XLA Ops:
  1.3 19.8 %shard_map.158 = (f32[2,128,512]{2,1,0:T(8,128)S(1)}, f32[2,512,512]{2,1,0:T(8,128)S(1)}, f32[2,2,512,256]{3,2,1,0:T(8,128)S(1)}, f32[2,2,128,256]{3,2,1,0:T(8,1...) custom-call(bf16[2,128,512]{2,1,0:T(8,128)(2,1)} %node_in.1, ...), custom_call_target="tpu_custom_call" | custom-call | tf_op jit(solution)/shard_map/pallas_call | solution.py:376
  21.1 3.0 %shard_map.159 = (bf16[2,128,512]{2,1,0:T(8,128)(2,1)}, bf16[2,512,512]{2,1,0:T(8,128)(2,1)}) custom-call(f32[2,128,512]{2,1,0:T(8,128)S(1)} %get-tuple-element.12.node_base, f32[2,512,512]{2,1,0:T(8,128)S(1)} %get-tuple-element.13.edge_base, f32[2,2,512,256]{3,2,1,0:T(8,128)S(1)} %get-tuple-element.14.pre, ...), custom_call_target="tpu_custom_call" | custom-call | tf_op jit(solution)/shard_map/pallas_call | solution.py:414

commit v3 on v2

--- a/solution.py
+++ b/solution.py
@@ -28,39 +28,63 @@
     return jnp.concatenate([dot(x, w[h]) for h in range(w.shape[0])], -1)
 
 
-def scaled(x, gain, live=None):
-    factor = lax.rsqrt(jnp.mean(x * x, -1, keepdims=True) + 1e-05)
-    if live is not None:
-        factor = jnp.where(live, factor, 0.0)
-    return x * factor * gain
+def scaled(x, gain):
+    return x * lax.rsqrt(jnp.mean(x * x, -1, keepdims=True) + 1e-05) * gain
 
 
 def live_rows(start, rows, count):
     return lax.broadcasted_iota(jnp.int32, (rows, 1), 0) + start < count
 
 
-def edge_rows(m, c, refs):
-    base, pre, table, gather, w2, gain, count, split = refs
-    rows = slice(c * CHUNK, (c + 1) * CHUNK)
-    hidden = jnp.concatenate(
-        [silu_of_half(pre[h, m, rows, :] + dot(gather[rows, split:], table[h, m, split:, :])) for h in range(2)], -1
-    )
-    update = scaled(wide_dot(hidden, w2), gain, live_rows(c * CHUNK, CHUNK, count))
-    return rows, (base[m, rows, :] + update).astype(BF16)
-
-
-def node_rows(base, pre, summed, refs):
+def node_chain(summed, base, pre, refs, finish):
     w3b, w4, gain = refs
-    hidden = jnp.concatenate([silu_of_half(pre[h] + 0.5 * dot(summed, w3b[h])) for h in range(2)], -1)
-    return (base + scaled(wide_dot(hidden, w4), gain)).astype(BF16)
+    total = summed()
+    yield
+    hidden = jnp.concatenate([silu_of_half(pre(h) + 0.5 * dot(total, w3b[h])) for h in range(2)], -1)
+    yield
+    finish((base() + scaled(wide_dot(hidden, w4), gain)).astype(BF16))
+
+
+def advance(chains):
+    return [chain for chain in chains if next(chain, chain) is None]
+
+
+def drain(chains):
+    while chains:
+        chains = advance(chains)
+
+
+def edge_pass(members, edges, refs, write, chain_of):
+    base, pre, table, gather, w2, gain, split = refs
+    items = [(m, c) for m in range(members) for c in range(edges // CHUNK)]
+
+    def hidden_of(m, c):
+        rows = slice(c * CHUNK, (c + 1) * CHUNK)
+        return jnp.concatenate(
+            [silu_of_half(pre[h, m, rows, :] + dot(gather[rows, split:], table[h, m, split:, :])) for h in range(2)], -1
+        )
+
+    ahead = hidden_of(*items[0])
+    chains = []
+    for i, (m, c) in enumerate(items):
+        hidden = ahead
+        if i + 1 < len(items):
+            ahead = hidden_of(*items[i + 1])
+        rows = slice(c * CHUNK, (c + 1) * CHUNK)
+        update = scaled(wide_dot(hidden, w2), gain)
+        write(m, rows, (base[m, rows, :] + update).astype(BF16))
+        chains = advance(chains)
+        if (c + 1) * CHUNK == edges:
+            chains.append(chain_of(m))
+    drain(chains)
 
 
 def exchange_kernel(
     sizes,
     node_in, edge_in, senders_in, receivers_in, counts_in, halo_in, long_in,
     ef_in, es_in, nf_in, ns_in, eg_in, eb_in, ng_in, nb_in,
-    node_base, edge_base, pre, node_pre, table, gather, scatter, weights, norms, count_row,
-    node, edge, first, ids_v, count_s, halo_v, long_v, picked, picker, sent_scatter, sent, sent_base, sent_pre, near, far_rows,
+    node_base, edge_base, pre, node_pre, table, gather, scatter, weights, norms,
+    node, edge, first, ids_v, count_s, halo_v, long_v, picked, picker, sent_scatter, sent, sent_base, sent_pre, near,
     halo_out, halo, far_out, far,
     node_sem, halo_sem, long_sem, ids_sem, count_sem, edge_sem, norm_sem,
     own_sem, ws_sem, wr_sem, hs_sem, hr_sem, fs_sem, fr_sem,
@@ -136,8 +160,30 @@
             start = 2 * side_rows + q * slots
             far_out[l, q, m] = packed[start : start + slots]
 
-    def send(l):
-        for side, step in ((1, 1), (0, n - 1)):
+    def partner_of(mask):
+        target, bit = 0, 1
+        while bit < n:
+            target = target + lax.rem(me // bit + (mask // bit) % 2, 2) * bit
+            bit *= 2
+        return target
+
+    if n & (n - 1):
+        targets = [lax.rem(me + step, n) for step in range(1, n)]
+    else:
+        targets = [partner_of(mask) for mask in range(n - 1, 0, -1)]
+
+    def send_far(l, some):
+        for target in some:
+            pltpu.make_async_remote_copy(
+                src_ref=far_out.at[l, target],
+                dst_ref=far.at[l, me],
+                send_sem=fs_sem.at[l],
+                recv_sem=fr_sem.at[l],
+                device_id={"dom": target},
+            ).start()
+
+    def send_halo(l):
+        for side, step in ((0, n - 1), (1, 1)):
             pltpu.make_async_remote_copy(
                 src_ref=halo_out.at[l, side],
                 dst_ref=halo.at[l, 1 - side],
@@ -145,15 +191,10 @@
                 recv_sem=hr_sem.at[l],
                 device_id={"dom": lax.rem(me + step, n)},
             ).start()
-        for step in range(1, n):
-            target = lax.rem(me + step, n)
-            pltpu.make_async_remote_copy(
-                src_ref=far_out.at[l, target],
-                dst_ref=far.at[l, me],
-                send_sem=fs_sem.at[l],
-                recv_sem=fr_sem.at[l],
-                device_id={"dom": target},
-            ).start()
+
+    def send(l):
+        send_halo(l)
+        send_far(l, targets)
         pltpu.make_async_copy(far_out.at[l, me], far.at[l, me], fr_sem.at[l]).start()
 
     whole(node, node_sem).wait()
@@ -175,6 +216,8 @@
             ).start()
 
     whole(ids_v, ids_sem).wait()
+    pltpu.make_async_copy(counts_in, count_s, count_sem).wait()
+    count = count_s[0]
     depth = gather.shape[1]
     senders = column(ids_v[0:1, :])
     receiver_row = ids_v[1:2, :]
@@ -182,7 +225,8 @@
     senders = jnp.where(senders < nodes, senders, senders + nodes)
     for c in range(depth // LANES):
         lane = lax.broadcasted_iota(jnp.int32, (edges, LANES), 1) + c * LANES
-        gather[:, c * LANES : (c + 1) * LANES] = one_hot((senders == lane) | (receivers == lane))
+        hits = ((senders == lane) | (receivers == lane)) & live_rows(0, edges, count)
+        gather[:, c * LANES : (c + 1) * LANES] = one_hot(hits)
     row = lax.broadcasted_iota(jnp.int32, (nodes, edges), 0)
     scatter[...] = one_hot(jnp.broadcast_to(receiver_row, (nodes, edges)) == row)
     sent_scatter[...] = dot(picker[...], scatter[...]).astype(BF16)
@@ -191,8 +235,6 @@
         for h in range(halves):
             for m in everyone:
                 table[h, m, far_base:, :] = jnp.zeros((depth - far_base, table.shape[3]), BF16)
-    pltpu.make_async_copy(counts_in, count_s, count_sem).wait()
-    count_row[...] = jnp.full(count_row.shape, count_s[0], jnp.int32)
     whole(edge, edge_sem).wait()
     whole(norms, norm_sem).wait()
 
@@ -216,8 +258,11 @@
         for m in everyone:
             for r in range(0, edges, LANES):
                 rows = slice(r, r + LANES)
-                live = live_rows(r, LANES, count_row[0:1, 0:1])
-                edge_base[m, rows, :] = jnp.where(live, edge[m, rows, :].astype(F32) + norms[1, l : l + 1, :], 0.0)
+                live = live_rows(r, LANES, count)
+                kept = edge[m, rows, :].astype(F32)
+                edge_base[m, rows, :] = jnp.where(live, kept + norms[1, l : l + 1, :], 0.0)
+                if l == 0:
+                    edge[m, rows, :] = jnp.where(live, kept, 0.0).astype(BF16)
 
     def node_prepare(l):
         centre(l, 0)
@@ -239,9 +284,7 @@
         for m in ms:
             for side in range(2):
                 near[m, side * side_rows : (side + 1) * side_rows, :] = halo[l, side, m]
-            for q in range(n):
-                far_rows[m, q * slots : (q + 1) * slots, :] = far[l, q, m].astype(F32)
-            near[m, 2 * side_rows :, :] = far_rows[m].astype(BF16)
+            near[m, 2 * side_rows :, :] = far[l, :, m].reshape(n * slots, width)
             for h in range(halves):
                 table[h, m, split : split + near_rows, :] = (
                     0.5 * dot(near[m], first[l, h, width : 2 * width, :])
@@ -267,24 +310,37 @@
         )
         edge_refs = (
             edge_base, pre, table, gather, w.at[:, :width],
-            norms[0, l : l + 1, :], count_row[0:1, 0:1], split,
+            norms[0, l : l + 1, :], split,
         )
-        for c in range(edges // CHUNK):
-            for m in everyone:
-                rows, value = edge_rows(m, c, edge_refs)
-                edge[m, rows, :] = value
-        summed = jnp.concatenate([dot(sent_scatter[...], edge[m]).astype(BF16) for m in everyone], 0)
-        started = [jnp.concatenate([sent_pre[m, h] for m in everyone], 0) for h in range(halves)]
-        fresh = node_rows(sent_base[...], started, summed, node_refs)
-        for m in everyone:
-            rows = fresh[m * near_rows : (m + 1) * near_rows]
-            if l + 1 < layers - 1:
-                sent[m] = rows
-            stage(l + 1, m, rows)
+
+        def write(m, rows, value):
+            edge[m, rows, :] = value
+
+        def sent_chain(m):
+            rows = slice(m * near_rows, (m + 1) * near_rows)
+
+            def finish(fresh):
+                if l + 1 < layers - 1:
+                    sent[m] = fresh
+                stage(l + 1, m, fresh)
+
+            return node_chain(
+                lambda: dot(sent_scatter[...], edge[m]).astype(BF16),
+                lambda: sent_base[rows, :], lambda h: sent_pre[m, h], node_refs, finish,
+            )
+
+        def kept_chain(m):
+            def finish(fresh):
+                node[m] = fresh
+
+            return node_chain(
+                lambda: dot(scatter[...], edge[m]).astype(BF16),
+                lambda: node_base[m], lambda h: node_pre[m, h], node_refs, finish,
+            )
+
+        edge_pass(members, edges, edge_refs, write, sent_chain)
         send(l + 1)
-        for m in everyone:
-            summed = dot(scatter[...], edge[m]).astype(BF16)
-            node[m] = node_rows(node_base[m], [node_pre[m, h] for h in range(halves)], summed, node_refs)
+        drain([kept_chain(m) for m in everyone])
         edge_prepare(l + 1)
         wait_weights(l + 1, 0)
         wait_partner(l + 1, 0)
@@ -303,7 +359,7 @@
 
 def finish_kernel(
     sizes,
-    node_base, edge_base, pre, node_pre, table, gather, scatter, weights, norms, count_row,
+    node_base, edge_base, pre, node_pre, table, gather, scatter, weights, norms,
     node_out, edge_out, edge_new, node_new, sem,
 ):
     n, layers, members, nodes, edges, width, side_rows, slots = sizes
@@ -316,28 +372,30 @@
         copy.start()
         copies.append(copy)
 
-    everyone = range(members)
-    halves = 2
     edge_refs = (
         edge_base, pre, table, gather, w.at[:, :width],
-        norms[0, l : l + 1, :], count_row[0:1, 0:1], 2 * nodes,
+        norms[0, l : l + 1, :], 2 * nodes,
     )
     node_refs = (
         w.at[:, 2 * width : 3 * width], w.at[:, 3 * width :],
         norms[2, l : l + 1, :],
     )
-    for c in range(edges // CHUNK):
-        for m in everyone:
-            rows, value = edge_rows(m, c, edge_refs)
-            edge_new[m, rows, :] = value
-            store(edge_new.at[m, rows], edge_out.at[m, rows])
-    summed = jnp.concatenate([dot(scatter[...], edge_new[m]).astype(BF16) for m in everyone], 0)
-    base = jnp.concatenate([node_base[m] for m in everyone], 0)
-    started = [jnp.concatenate([node_pre[m, h] for m in everyone], 0) for h in range(halves)]
-    fresh = node_rows(base, started, summed, node_refs)
-    for m in everyone:
-        node_new[m] = fresh[m * nodes : (m + 1) * nodes]
-    store(node_new, node_out)
+
+    def write(m, rows, value):
+        edge_new[m, rows, :] = value
+        store(edge_new.at[m, rows], edge_out.at[m, rows])
+
+    def chain_of(m):
+        def finish(fresh):
+            node_new[m] = fresh
+            store(node_new.at[m], node_out.at[m])
+
+        return node_chain(
+            lambda: dot(scatter[...], edge_new[m]).astype(BF16),
+            lambda: node_base[m], lambda h: node_pre[m, h], node_refs, finish,
+        )
+
+    edge_pass(members, edges, edge_refs, write, chain_of)
     for copy in copies:
         copy.wait()
 
@@ -371,7 +429,6 @@
             ((nodes, edges), BF16),
             ((layers, 2, 4 * width, half), BF16),
             ((4,) + eg.shape, F32),
-            ((1, LANES), jnp.int32),
         ]
         state = pl.pallas_call(
             functools.partial(exchange_kernel, sizes),
@@ -393,7 +450,6 @@
                 pltpu.VMEM((members * near_rows, width), F32),
                 pltpu.VMEM((members, 2, near_rows, half), F32),
                 pltpu.VMEM((members, near_rows, width), BF16),
-                pltpu.VMEM((members, n * slots, width), F32),
                 pltpu.VMEM((layers, 2, members, side_rows, width), BF16),
                 pltpu.VMEM((layers, 2, members, side_rows, width), BF16),
                 pltpu.VMEM((layers, n, members, slots, width), BF16),
@@ -422,7 +478,7 @@
             scratch_shapes=[
                 pltpu.VMEM(edge.shape, BF16),
                 pltpu.VMEM(node.shape, BF16),
-                dma((1 + members * (edges // CHUNK),)),
+                dma((members * (1 + edges // CHUNK),)),
             ],
             compiler_params=pltpu.CompilerParams(vmem_limit_bytes=40 * 1024 * 1024),
         )(*state)

time: 24.3 us -> 23.4 us (0.963)
  Pallas kernels: 22.8 us -> 21.9 us
    pallas_call x1, Pallas kernels: 19.8 us -> 19.2 us  [step(): pl.pallas_call(functools.partial(exchange_kernel, sizes), out_shape=tuple...]
    pallas_call x1, Pallas kernels: 2.98 us -> 2.67 us  [step(): pl.pallas_call(functools.partial(finish_kernel, sizes), out_shape=(jax.Sh...]
where the time goes in v3:
time: 23.4 us; the launch traced here: 23.2 us
  Pallas kernels  21.9 us (94%)
  between operations  1.29 us (6%)
    pallas_call x1, Pallas kernels, step(): pl.pallas_call(functools.partial(exchange_kernel, sizes), out_shape=tuple...  19.2 us
    pallas_call x1, Pallas kernels, step(): pl.pallas_call(functools.partial(finish_kernel, sizes), out_shape=(jax.Sh...  2.67 us

profile of v3, /device:TPU:0, one launch (start us, length us, event | category | flops | bytes accessed | tf_op | source)
XLA Modules:
  0.0 23.2 jit_solution(13188804198687305274)
XLA Ops:
  1.3 19.2 %shard_map.158 = (f32[2,128,512]{2,1,0:T(8,128)S(1)}, f32[2,512,512]{2,1,0:T(8,128)S(1)}, f32[2,2,512,256]{3,2,1,0:T(8,128)S(1)}, f32[2,2,128,256]{3,2,1,0:T(8,1...) custom-call(bf16[2,128,512]{2,1,0:T(8,128)(2,1)} %node_in.1, ...), custom_call_target="tpu_custom_call" | custom-call | tf_op jit(solution)/shard_map/pallas_call | solution.py:433
  20.5 2.7 %shard_map.159 = (bf16[2,128,512]{2,1,0:T(8,128)(2,1)}, bf16[2,512,512]{2,1,0:T(8,128)(2,1)}) custom-call(f32[2,128,512]{2,1,0:T(8,128)S(1)} %get-tuple-element.11.node_base, f32[2,512,512]{2,1,0:T(8,128)S(1)} %get-tuple-element.12.edge_base, f32[2,2,512,256]{3,2,1,0:T(8,128)S(1)} %get-tuple-element.13.pre, ...), custom_call_target="tpu_custom_call" | custom-call | tf_op jit(solution)/shard_map/pallas_call | solution.py:470

commit v4 on v3

--- a/solution.py
+++ b/solution.py
@@ -79,15 +79,15 @@
     drain(chains)
 
 
-def exchange_kernel(
+def exchange_body(
     sizes,
     node_in, edge_in, senders_in, receivers_in, counts_in, halo_in, long_in,
     ef_in, es_in, nf_in, ns_in, eg_in, eb_in, ng_in, nb_in,
     node_base, edge_base, pre, node_pre, table, gather, scatter, weights, norms,
-    node, edge, first, ids_v, count_s, halo_v, long_v, picked, picker, sent_scatter, sent, sent_base, sent_pre, near,
-    halo_out, halo, far_out, far,
-    node_sem, halo_sem, long_sem, ids_sem, count_sem, edge_sem, norm_sem,
-    own_sem, ws_sem, wr_sem, hs_sem, hr_sem, fs_sem, fr_sem,
+    node, edge, first, ids_v, count_s, halo_v, long_v, picked, picker, sent_scatter, sent, sent_base, sent_pre,
+    outgoing, incoming,
+    wr_sem, in_sem,
+    node_sem, halo_sem, long_sem, ids_sem, count_sem, edge_sem, norm_sem, own_sem, ws_sem, out_sem,
 ):
     n, layers, members, nodes, edges, width, side_rows, slots = sizes
     me = lax.axis_index("dom")
@@ -153,12 +153,10 @@
         lane = lax.broadcasted_iota(jnp.int32, picked.shape, 1) + c * LANES
         picker[:, c * LANES : (c + 1) * LANES] = one_hot(picked[...] == lane)
 
+    span = side_rows // slots
+
     def stage(l, m, packed):
-        for side in range(2):
-            halo_out[l, side, m] = packed[side * side_rows : (side + 1) * side_rows]
-        for q in range(n):
-            start = 2 * side_rows + q * slots
-            far_out[l, q, m] = packed[start : start + slots]
+        outgoing[l, :, m] = packed.reshape(2 * span + n, slots, width)
 
     def partner_of(mask):
         target, bit = 0, 1
@@ -172,30 +170,20 @@
     else:
         targets = [partner_of(mask) for mask in range(n - 1, 0, -1)]
 
-    def send_far(l, some):
-        for target in some:
+    def send(l):
+        pieces = [(side * span, (1 - side) * span, span, lax.rem(me + step, n)) for side, step in ((0, n - 1), (1, 1))]
+        pieces += [(2 * span + target, 2 * span + me, 1, target) for target in targets]
+        pieces = pieces[2:3] + pieces[:2] + pieces[3:]
+        for start, landing, count, target in pieces:
             pltpu.make_async_remote_copy(
-                src_ref=far_out.at[l, target],
-                dst_ref=far.at[l, me],
-                send_sem=fs_sem.at[l],
-                recv_sem=fr_sem.at[l],
+                src_ref=outgoing.at[l, pl.ds(start, count)],
+                dst_ref=incoming.at[l, pl.ds(landing, count)],
+                send_sem=out_sem.at[l],
+                recv_sem=in_sem.at[l],
                 device_id={"dom": target},
             ).start()
-
-    def send_halo(l):
-        for side, step in ((0, n - 1), (1, 1)):
-            pltpu.make_async_remote_copy(
-                src_ref=halo_out.at[l, side],
-                dst_ref=halo.at[l, 1 - side],
-                send_sem=hs_sem.at[l],
-                recv_sem=hr_sem.at[l],
-                device_id={"dom": lax.rem(me + step, n)},
-            ).start()
-
-    def send(l):
-        send_halo(l)
-        send_far(l, targets)
-        pltpu.make_async_copy(far_out.at[l, me], far.at[l, me], fr_sem.at[l]).start()
+        mine = pl.ds(2 * span + me, 1)
+        pltpu.make_async_copy(outgoing.at[l, mine], incoming.at[l, mine], in_sem.at[l]).start()
 
     whole(node, node_sem).wait()
     for m in everyone:
@@ -210,7 +198,7 @@
             pltpu.make_async_remote_copy(
                 src_ref=src,
                 dst_ref=dst,
-                send_sem=ws_sem.at[l, min(k, 1)],
+                send_sem=ws_sem.at[min(k, 1)],
                 recv_sem=wr_sem.at[l, min(k, 1)],
                 device_id={"mem": other},
             ).start()
@@ -279,15 +267,12 @@
                 node_pre[m, h] = 0.5 * dot(node[m], w3a)
 
     def receive(l, ms):
-        whole(far.at[l], fr_sem.at[l]).wait()
-        whole(halo.at[l], hr_sem.at[l]).wait()
+        whole(incoming.at[l], in_sem.at[l]).wait()
         for m in ms:
-            for side in range(2):
-                near[m, side * side_rows : (side + 1) * side_rows, :] = halo[l, side, m]
-            near[m, 2 * side_rows :, :] = far[l, :, m].reshape(n * slots, width)
+            near = incoming[l, :, m].reshape(near_rows, width)
             for h in range(halves):
                 table[h, m, split : split + near_rows, :] = (
-                    0.5 * dot(near[m], first[l, h, width : 2 * width, :])
+                    0.5 * dot(near, first[l, h, width : 2 * width, :])
                 ).astype(BF16)
 
     edge_prepare(0)
@@ -350,28 +335,26 @@
         wait_partner(l + 1, 1)
         node_prepare(l + 1)
 
+    whole(first.at[:, core], ws_sem.at[0]).wait()
+    whole(weights.at[:, core], ws_sem.at[1]).wait()
     for l in range(layers):
-        whole(first.at[l, core], ws_sem.at[l, 0]).wait()
-        whole(weights.at[l, core], ws_sem.at[l, 1]).wait()
-        whole(far_out.at[l, : n - 1], fs_sem.at[l]).wait()
-        whole(halo_out.at[l], hs_sem.at[l]).wait()
-
-
-def finish_kernel(
+        whole(outgoing.at[l, : 2 * span + n - 1], out_sem.at[l]).wait()
+
+
+def exchange_kernel(sizes, *refs):
+    layers, dma = sizes[1], pltpu.SemaphoreType.DMA
+    local = [dma(())] * 7 + [dma((layers, 2)), dma((2,)), dma((layers,))]
+    pl.run_scoped(functools.partial(exchange_body, sizes, *refs), *local)
+
+
+def finish_body(
     sizes,
     node_base, edge_base, pre, node_pre, table, gather, scatter, weights, norms,
-    node_out, edge_out, edge_new, node_new, sem,
+    node_out, edge_out, edge_new, node_new, edge_sem, node_sem,
 ):
     n, layers, members, nodes, edges, width, side_rows, slots = sizes
     l = layers - 1
     w = weights.at[l]
-    copies = []
-
-    def store(src, dst):
-        copy = pltpu.make_async_copy(src, dst, sem.at[len(copies)])
-        copy.start()
-        copies.append(copy)
-
     edge_refs = (
         edge_base, pre, table, gather, w.at[:, :width],
         norms[0, l : l + 1, :], 2 * nodes,
@@ -383,12 +366,12 @@
 
     def write(m, rows, value):
         edge_new[m, rows, :] = value
-        store(edge_new.at[m, rows], edge_out.at[m, rows])
+        pltpu.make_async_copy(edge_new.at[m, rows], edge_out.at[m, rows], edge_sem).start()
 
     def chain_of(m):
         def finish(fresh):
             node_new[m] = fresh
-            store(node_new.at[m], node_out.at[m])
+            pltpu.make_async_copy(node_new.at[m], node_out.at[m], node_sem).start()
 
         return node_chain(
             lambda: dot(scatter[...], edge_new[m]).astype(BF16),
@@ -396,8 +379,13 @@
         )
 
     edge_pass(members, edges, edge_refs, write, chain_of)
-    for copy in copies:
-        copy.wait()
+    pltpu.make_async_copy(edge_new, edge_out, edge_sem).wait()
+    pltpu.make_async_copy(node_new, node_out, node_sem).wait()
+
+
+def finish_kernel(sizes, *refs):
+    dma = pltpu.SemaphoreType.DMA
+    pl.run_scoped(functools.partial(finish_body, sizes, *refs), dma(()), dma(()))
 
 
 def solution(mesh):
@@ -449,18 +437,9 @@
                 pltpu.VMEM((members, near_rows, width), BF16),
                 pltpu.VMEM((members * near_rows, width), F32),
                 pltpu.VMEM((members, 2, near_rows, half), F32),
-                pltpu.VMEM((members, near_rows, width), BF16),
-                pltpu.VMEM((layers, 2, members, side_rows, width), BF16),
-                pltpu.VMEM((layers, 2, members, side_rows, width), BF16),
-                pltpu.VMEM((layers, n, members, slots, width), BF16),
-                pltpu.VMEM((layers, n, members, slots, width), BF16),
-            ] + [dma(())] * 7 + [
+                pltpu.VMEM((layers, near_rows // slots, members, slots, width), BF16),
+                pltpu.VMEM((layers, near_rows // slots, members, slots, width), BF16),
                 dma((layers, 2)),
-                dma((layers, 2)),
-                dma((layers, 2)),
-                dma((layers,)),
-                dma((layers,)),
-                dma((layers,)),
                 dma((layers,)),
             ],
             compiler_params=pltpu.CompilerParams(
@@ -478,7 +457,6 @@
             scratch_shapes=[
                 pltpu.VMEM(edge.shape, BF16),
                 pltpu.VMEM(node.shape, BF16),
-                dma((members * (1 + edges // CHUNK),)),
             ],
             compiler_params=pltpu.CompilerParams(vmem_limit_bytes=40 * 1024 * 1024),
         )(*state)

time: 23.4 us -> 23.1 us (0.987)
  Pallas kernels: 21.9 us -> 21.6 us
where the time goes in v4:
time: 23.1 us; the launch traced here: 22.9 us
  Pallas kernels  21.6 us (94%)
  between operations  1.29 us (6%)
    pallas_call x1, Pallas kernels, step(): pl.pallas_call(functools.partial(exchange_kernel, sizes), out_shape=tuple...  19 us
    pallas_call x1, Pallas kernels, step(): pl.pallas_call(functools.partial(finish_kernel, sizes), out_shape=(jax.Sh...  2.61 us

profile of v4, /device:TPU:0, one launch (start us, length us, event | category | flops | bytes accessed | tf_op | source)
XLA Modules:
  0.0 22.9 jit_solution(11763764225325680727)
XLA Ops:
  1.3 19.0 %shard_map.158 = (f32[2,128,512]{2,1,0:T(8,128)S(1)}, f32[2,512,512]{2,1,0:T(8,128)S(1)}, f32[2,2,512,256]{3,2,1,0:T(8,128)S(1)}, f32[2,2,128,256]{3,2,1,0:T(8,1...) custom-call(bf16[2,128,512]{2,1,0:T(8,128)(2,1)} %refs_0_.1, ...), custom_call_target="tpu_custom_call" | custom-call | tf_op jit(solution)/shard_map/pallas_call | solution.py:421
  20.3 2.6 %shard_map.159 = (bf16[2,128,512]{2,1,0:T(8,128)(2,1)}, bf16[2,512,512]{2,1,0:T(8,128)(2,1)}) custom-call(f32[2,128,512]{2,1,0:T(8,128)S(1)} %get-tuple-element.11.refs_0_, f32[2,512,512]{2,1,0:T(8,128)S(1)} %get-tuple-element.12.refs_1_, f32[2,2,512,256]{3,2,1,0:T(8,128)S(1)} %get-tuple-element.13.refs_2_, ...), custom_call_target="tpu_custom_call" | custom-call | tf_op jit(solution)/shard_map/pallas_call | solution.py:449

commit v5 on v4

--- a/solution.py
+++ b/solution.py
@@ -56,25 +56,26 @@
 
 def edge_pass(members, edges, refs, write, chain_of):
     base, pre, table, gather, w2, gain, split = refs
-    items = [(m, c) for m in range(members) for c in range(edges // CHUNK)]
-
-    def hidden_of(m, c):
-        rows = slice(c * CHUNK, (c + 1) * CHUNK)
+    cuts = [slice(r, r + CHUNK) for r in range(0, edges, CHUNK)]
+    middle = edges - CHUNK // 2
+    items = [(m, rows) for m in range(members) for rows in cuts]
+    items[-1:] = [(members - 1, slice(edges - CHUNK, middle)), (members - 1, slice(middle, edges))]
+
+    def hidden_of(m, rows):
         return jnp.concatenate(
             [silu_of_half(pre[h, m, rows, :] + dot(gather[rows, split:], table[h, m, split:, :])) for h in range(2)], -1
         )
 
     ahead = hidden_of(*items[0])
     chains = []
-    for i, (m, c) in enumerate(items):
+    for i, (m, rows) in enumerate(items):
         hidden = ahead
         if i + 1 < len(items):
             ahead = hidden_of(*items[i + 1])
-        rows = slice(c * CHUNK, (c + 1) * CHUNK)
         update = scaled(wide_dot(hidden, w2), gain)
         write(m, rows, (base[m, rows, :] + update).astype(BF16))
         chains = advance(chains)
-        if (c + 1) * CHUNK == edges:
+        if rows.stop == edges:
             chains.append(chain_of(m))
     drain(chains)
 

time: 23.1 us -> 23.1 us (level)
  no operation moved by 1% of the time
where the time goes in v5:
time: 23.1 us; the launch traced here: 22.9 us
  Pallas kernels  21.6 us (94%)
  between operations  1.29 us (6%)
    pallas_call x1, Pallas kernels, step(): pl.pallas_call(functools.partial(exchange_kernel, sizes), out_shape=tuple...  19 us
    pallas_call x1, Pallas kernels, step(): pl.pallas_call(functools.partial(finish_kernel, sizes), out_shape=(jax.Sh...  2.62 us

profile of v5, /device:TPU:0, one launch (start us, length us, event | category | flops | bytes accessed | tf_op | source)
XLA Modules:
  0.0 22.9 jit_solution(13588869092246517193)
XLA Ops:
  1.3 19.0 %shard_map.158 = (f32[2,128,512]{2,1,0:T(8,128)S(1)}, f32[2,512,512]{2,1,0:T(8,128)S(1)}, f32[2,2,512,256]{3,2,1,0:T(8,128)S(1)}, f32[2,2,128,256]{3,2,1,0:T(8,1...) custom-call(bf16[2,128,512]{2,1,0:T(8,128)(2,1)} %refs_0_.1, ...), custom_call_target="tpu_custom_call" | custom-call | tf_op jit(solution)/shard_map/pallas_call | solution.py:422
  20.3 2.6 %shard_map.159 = (bf16[2,128,512]{2,1,0:T(8,128)(2,1)}, bf16[2,512,512]{2,1,0:T(8,128)(2,1)}) custom-call(f32[2,128,512]{2,1,0:T(8,128)S(1)} %get-tuple-element.11.refs_0_, f32[2,512,512]{2,1,0:T(8,128)S(1)} %get-tuple-element.12.refs_1_, f32[2,2,512,256]{3,2,1,0:T(8,128)S(1)} %get-tuple-element.13.refs_2_, ...), custom_call_target="tpu_custom_call" | custom-call | tf_op jit(solution)/shard_map/pallas_call | solution.py:450
